TPU v7x, 32 devices: a whole 2x2x4 slice. The times are simulated.
32 devices in a mesh: rows: 4 (over z), bundle: 8 (over y, x, core).
Axes of the slice: x: 2, y: 2, z: 4, core: 2. Of those that a mesh axis runs over, the one named last changes fastest.
Arguments:
- raw_values: float32 [8192, 4096], P(('rows', 'bundle')), may hold values from -2100 to 2100
- bin_edges: float32 [4096, 255], P(('rows', 'bundle')), may hold values from -2100 to 2100, as said below
- feature_column: int32 [4096], replicated, may hold values from 0 to 4095, each once
- bin_offset: int32 [4096], replicated, may hold values from 0 to 63
Outputs:
- bin_codes: int32 [8192, 4096], P('rows', 'bundle')
Inputs may be any that keep to these rules, and one draw needn't show every extreme that they name: Every row of bin_edges is strictly increasing. `feature_column`: each column 0 .. 4095 is named once.
All inputs are finite; a program needn't handle non-finite values.
Results may differ from a plain program's by a relative error of at most 0.0003.
Values may be sent and summed in bfloat16 or wider, within the bound.
A program may use at most 64 MiB of HBM per device.

v0:
```python
import math

import jax
import jax.numpy as jnp
from jax import lax
from jax.sharding import PartitionSpec as P


def count_below(values, edges):
    total = values.shape[0]
    block = math.gcd(total, 512)

    def one_block(part_rows):
        return jnp.sum(part_rows[:, :, None] > edges[None, :, :], axis=2, dtype=jnp.int32)

    blocks = values.reshape(total // block, block, values.shape[1])
    return lax.map(one_block, blocks).reshape(total, values.shape[1])


def local(raw_values, bin_edges, feature_column, bin_offset):
    count_feat = feature_column.shape[0]
    owner_feature = (
        jnp.zeros((count_feat,), jnp.int32)
        .at[feature_column]
        .set(jnp.arange(count_feat, dtype=jnp.int32))
    )
    edges_all = lax.all_gather(bin_edges, ("rows", "bundle"), axis=0, tiled=True)
    span_cols = count_feat // lax.axis_size("bundle")
    first_col = lax.axis_index("bundle") * span_cols
    owned_features = lax.dynamic_slice_in_dim(owner_feature, first_col, span_cols, 0)
    owned_offsets = jnp.take(bin_offset, owned_features)
    ordered = jnp.take(raw_values, owner_feature, axis=1)
    arrived = lax.all_to_all(ordered, "bundle", split_axis=1, concat_axis=0, tiled=True)
    owned_edges = jnp.take(edges_all, owned_features, axis=0)
    bins = count_below(arrived, owned_edges)
    return bins + owned_offsets[None, :]


def solution(mesh):
    in_specs = (P(("rows", "bundle"), None), P(("rows", "bundle"), None), P(), P())
    out_specs = P("rows", "bundle")
    return jax.shard_map(local, mesh=mesh, in_specs=in_specs, out_specs=out_specs, check_vma=False)
```

profile of v0, /device:TPU:0, one launch (start us, length us, event | category | flops | bytes accessed | tf_op | source)
XLA Modules:
  0.0 272.0 jit_solution(10989593303476513043)
XLA Ops:
  6.5 0.7 all-gather.2.cloned.1.call-update
  7.3 5.6 %copy.9 = f32[256,4096]{0,1:T(8,128)} copy(f32[256,4096]{1,0:T(8,128)} %param.6) | data formatting | bytes 8388608 | tf_op args[0]
  12.9 15.5 %scatter_custom_fusion = s32[4096]{0:T(1024)S(1)} fusion(s32[4096]{0:T(1024)S(1)} %compare_select_fusion.1, s32[4096]{0:T(1024)S(1)} %iota.3, s32[]{:T(128)} %copy.20), kind=kCustom, calls=%fused_computation.14 | custom fusion | bytes 16388 | tf_op jit(solution)/shard_map/scatter | solution.py:25
  28.5 18.4 %gather_fusion = f32[4096,256]{1,0:T(8,128)} fusion(f32[256,4096]{0,1:T(8,128)} %copy.9, s32[4096]{0:T(1024)S(1)} %fusion), kind=kCustom, calls=%fused_computation | custom fusion | bytes 8404992 | tf_op jit(solution)/shard_map/jit(_take)/gather | solution.py:32
  46.9 3.9 %broadcast_select_fusion = f32[256,8,512]{0,2,1:T(8,128)} fusion(f32[256,8,512]{0,2,1:T(8,128)} %bitcast.16, pred[8,512]{1,0:T(8,128)(4,1)S(1)} %broadcast_in_dim.47), kind=kLoop, calls=%fused_computation.8 | loop fusion | flops 1048576 | bytes 8392704 | tf_op jit(solution)/shard_map/jit(_take)/select_n | solution.py:32
  50.8 5.2 %all-to-all-start = ((f32[256,8,512]{0,2,1:T(8,128)}), f32[256,8,512]{0,2,1:T(8,128)}, u32[]{:S(2)}, u32[]{:S(2)}) async-start(f32[256,8,512]{0,2,1:T(8,128)} %broadcast_select_fusion), calls=%async_computation | async-start | bytes 8388608 | tf_op jit(solution)/shard_map/all_to_all | solution.py:33
  56.1 3.1 %gather_fusion.2 = s32[512]{0:T(512)S(1)} fusion(s32[4096]{0:T(1024)S(1)} %copy-done, s32[1024]{0:T(1024)S(1)} %pad_clamp_fusion), kind=kCustom, calls=%fused_computation.2 | custom fusion | bytes 6144 | tf_op jit(solution)/shard_map/jit(_take)/gather | solution.py:31
  59.3 52.5 %all-to-all-done = f32[256,8,512]{0,2,1:T(8,128)} async-done(((f32[256,8,512]{0,2,1:T(8,128)}), f32[256,8,512]{0,2,1:T(8,128)}, u32[]{:S(2)}, u32[]{:S(2)}) %all-to-all-start) | async-done | bytes 4194336 | tf_op jit(solution)/shard_map/all_to_all | solution.py:33
  111.8 5.3 %copy.10 = f32[8,256,512]{2,1,0:T(8,128)} copy(f32[8,256,512]{1,2,0:T(8,128)} %bitcast.4) | data formatting | bytes 8388608 | tf_op jit(solution)/shard_map/all_to_all | solution.py:33
  117.1 3.8 %gather_fusion.1 = f32[512,255]{1,0:T(8,128)S(1)} fusion(f32[4096,255]{1,0:T(8,128)} %all-gather.2.cloned.1.call-done, s32[1024]{0:T(1024)S(1)} %pad_clamp_fusion), kind=kCustom, calls=%fused_computation.1 | custom fusion | bytes 1046528 | tf_op jit(solution)/shard_map/jit(_take)/gather | solution.py:34
  121.3 139.2 %while.10 = (s32[]{:T(128)}, s32[4,512,512]{2,1,0:T(8,128)}, f32[4,512,512]{2,1,0:T(8,128)}, f32[512,255]{0,1:T(8,128)S(1)}, s32[]{:T(128)}) while((s32[]{:T(128)}, s32[4,512,512]{2,1,0:T(8,128)}, f32[4,512,512]{2,1,0:T(8,128)}, f32[512,255]{0,1:T(8,128)S(1)}, s32[]{:T(128)}) %tuple.25), condition=%wide.region_3.4_spmd, body=%wide.region_1.0_spmd.sunk | while | flops 200278016 | bytes 6814273 | solution.py:17
  121.3 1.3 dynamic-slice_bitcast_fusion.2
  122.6 32.4 %convert_reduce_fusion.2 = s32[512,512]{1,0:T(8,128)S(1)} fusion(f32[512,255]{0,1:T(8,128)S(1)} %get-tuple-element.80, f32[512,512]{1,0:T(8,128)S(1)} %dynamic-slice_bitcast_fusion.2), kind=kLoop, calls=%fused_computation.4.clone.1 | loop fusion | flops 200278016 | bytes 2619392 | tf_op jit(solution)/shard_map/while/body/eval_jaxpr/reduce_sum | solution.py:14
  155.0 1.1 bitcast_dynamic-update-slice_fusion.2
  156.0 1.3 dynamic-slice_bitcast_fusion.2
  157.3 32.4 %convert_reduce_fusion.2 = s32[512,512]{1,0:T(8,128)S(1)} fusion(f32[512,255]{0,1:T(8,128)S(1)} %get-tuple-element.80, f32[512,512]{1,0:T(8,128)S(1)} %dynamic-slice_bitcast_fusion.2), kind=kLoop, calls=%fused_computation.4.clone.1 | loop fusion | flops 200278016 | bytes 2619392 | tf_op jit(solution)/shard_map/while/body/eval_jaxpr/reduce_sum | solution.py:14
  189.8 1.1 bitcast_dynamic-update-slice_fusion.2
  190.8 1.3 dynamic-slice_bitcast_fusion.2
  192.1 32.4 %convert_reduce_fusion.2 = s32[512,512]{1,0:T(8,128)S(1)} fusion(f32[512,255]{0,1:T(8,128)S(1)} %get-tuple-element.80, f32[512,512]{1,0:T(8,128)S(1)} %dynamic-slice_bitcast_fusion.2), kind=kLoop, calls=%fused_computation.4.clone.1 | loop fusion | flops 200278016 | bytes 2619392 | tf_op jit(solution)/shard_map/while/body/eval_jaxpr/reduce_sum | solution.py:14
  224.6 1.1 bitcast_dynamic-update-slice_fusion.2
  225.6 1.3 dynamic-slice_bitcast_fusion.2
  226.9 32.4 %convert_reduce_fusion.2 = s32[512,512]{1,0:T(8,128)S(1)} fusion(f32[512,255]{0,1:T(8,128)S(1)} %get-tuple-element.80, f32[512,512]{1,0:T(8,128)S(1)} %dynamic-slice_bitcast_fusion.2), kind=kLoop, calls=%fused_computation.4.clone.1 | loop fusion | flops 200278016 | bytes 2619392 | tf_op jit(solution)/shard_map/while/body/eval_jaxpr/reduce_sum | solution.py:14
  259.3 1.1 bitcast_dynamic-update-slice_fusion.2
  260.4 4.7 %bitcast_add_fusion = s32[2048,512]{1,0:T(8,128)} fusion(s32[4,512,512]{2,1,0:T(8,128)} %get-tuple-element.27, s32[512]{0:T(512)S(1)} %get-tuple-element.40), kind=kLoop, calls=%fused_computation.7 | loop fusion | flops 1048576 | bytes 8390656 | tf_op jit(solution)/shard_map/add | solution.py:36
  (17 shorter events, 0.6 us)
Async XLA Ops:
  6.5 49.5 %copy-start = (s32[4096]{0:T(1024)S(1)}, s32[4096]{0:T(1024)}, u32[]{:S(2)}) copy-start(s32[4096]{0:T(1024)} %param.9) | copy-start | bytes 49156
  6.5 110.6 %all-gather.2.cloned.1.call-start = ((), (), s32[]{:S(2)}) async-start(), calls=%async_computation.1 | async-start | bytes 4325376 | tf_op jit(solution)/shard_map/all_gather | solution.py:27
  7.3 5.6 %copy-start.1 = (s32[4096]{0:T(1024)S(1)}, s32[4096]{0:T(1024)}, u32[]{:S(2)}) copy-start(s32[4096]{0:T(1024)} %param.8) | copy-start | bytes 49156
  50.8 61.0 %all-to-all-start = ((f32[256,8,512]{0,2,1:T(8,128)}), f32[256,8,512]{0,2,1:T(8,128)}, u32[]{:S(2)}, u32[]{:S(2)}) async-start(f32[256,8,512]{0,2,1:T(8,128)} %broadcast_select_fusion), calls=%async_computation | async-start | bytes 8388608 | tf_op jit(solution)/shard_map/all_to_all | solution.py:33
Sparse Core Ops, SparseCore 0:
  10.2 69.3 all-gather.1
where the time goes:
time: 273 us; the launch traced here: 272 us
  other arithmetic  139 us (51%)
  local copies, waits for them, and re-layouts  61.4 us (22%)
  waiting for transfers between devices  53.2 us (19%)
  between operations  13.5 us (5%)
  starting transfers between devices  5.2 us (2%)
    reduce_sum x4, other arithmetic, one_block(): jnp.sum(part_rows[:, :, None] > edges[None, :, :], axis=2, dtype=jnp.int32)  130 us
    all_to_all x1, waiting for transfers between devices, local(): lax.all_to_all(ordered, 'bundle', split_axis=1, concat_axis=0, tiled=True)  52.5 us
    gather x1, local copies, waits for them, and re-layouts, local(): ordered = jnp.take(raw_values, owner_feature, axis=1)  18.4 us
    scatter x1, local copies, waits for them, and re-layouts, local(): owner_feature = jnp.zeros((count_feat,), jnp.int32).at[feature_column].se...  15.5 us
    unnamed x5, local copies, waits for them, and re-layouts  5.61 us
  transfers between devices with their start and end apart: 2, of which 1 were waited for; matrix products, arithmetic and copies ran while one was open for 19% of the time, Pallas kernels for 0%

commit v1 on v0

v1 whole, which is shorter than its diff:
```python
import functools

import jax
import jax.numpy as jnp
from jax import lax
from jax.experimental import pallas as pl
from jax.experimental.pallas import tpu as pltpu
from jax.sharding import PartitionSpec as P

LANES = 128


def lane_gather(table, index):
    return jnp.take_along_axis(table, index, axis=1, mode="promise_in_bounds")


def table_kernel(edges_ref, offset_ref, table_ref):
    low, high = edges_ref[:, :LANES], edges_ref[:, LANES:]
    lane = lax.broadcasted_iota(jnp.int32, low.shape, 1)
    edge = jnp.zeros_like(lane)
    for level in range(7):
        width = 1 << level
        at_level = (lane >= width) & (lane < 2 * width)
        edge = jnp.where(at_level, (2 * (lane - width) + 1) * (LANES // width) - 1, edge)

    def pick(index):
        inner = index & (LANES - 1)
        return jnp.where(index < LANES, lane_gather(low, inner), lane_gather(high, inner))

    offset = jnp.broadcast_to(offset_ref[...], low.shape)
    table_ref[:, :LANES] = jnp.where(lane == 0, offset, pick(edge))
    table_ref[:, LANES:] = pick(2 * lane)


def make_tables(edges, offsets):
    count = edges.shape[0]
    return pl.pallas_call(
        table_kernel,
        out_shape=jax.ShapeDtypeStruct((count, 2 * LANES), jnp.float32),
        name="make_tables",
    )(jnp.pad(edges, ((0, 0), (0, 2 * LANES - edges.shape[1]))), offsets)


def bin_kernel(column_ref, raw_ref, table_ref, code_ref):
    features = raw_ref.shape[1]
    first = pl.program_id(0) * features
    group = 64
    for start in range(0, features, group):
        values = raw_ref[:, start : start + group].T
        tree = table_ref[start : start + group, :LANES]
        leaves = table_ref[start : start + group, LANES:]
        root = jnp.broadcast_to(tree[:, 1:2], tree.shape)
        halves = []
        for half in range(2):
            x = values[:, half * LANES : (half + 1) * LANES]
            node = jnp.where(x > root, 3, 2)
            for _ in range(6):
                node = 2 * node + jnp.where(x > lane_gather(tree, node), 1, 0)
            leaf = node - LANES
            halves.append(2 * leaf + jnp.where(x > lane_gather(leaves, leaf), 1, 0))
        offset = jnp.broadcast_to(tree[:, 0:1], tree.shape).astype(jnp.int32)
        packed = halves[0] + halves[1] * 65536 + offset * 65537
        for row in range(group):
            column = column_ref[first + start + row]
            code_ref[pl.ds(column, 1), :] = packed[row : row + 1, :]


def bin_rows(column, raw, tables):
    rows, features = raw.shape
    block = 128
    return pl.pallas_call(
        bin_kernel,
        grid_spec=pltpu.PrefetchScalarGridSpec(
            num_scalar_prefetch=1,
            grid=(features // block,),
            in_specs=[
                pl.BlockSpec((rows, block), lambda i, c: (0, i)),
                pl.BlockSpec((block, 2 * LANES), lambda i, c: (i, 0)),
            ],
            out_specs=pl.BlockSpec((features, rows // 2), lambda i, c: (0, 0)),
        ),
        out_shape=jax.ShapeDtypeStruct((features, rows // 2), jnp.int32),
        name="bin_rows",
    )(column, raw, tables)


def unpack_kernel(code_ref, out_ref):
    half = code_ref.shape[2]
    codes = code_ref[0].T
    out_ref[:half, :] = codes & 65535
    out_ref[half:, :] = codes >> 16


def unpack(codes):
    sources, columns, half = codes.shape
    return pl.pallas_call(
        unpack_kernel,
        grid=(sources,),
        in_specs=[pl.BlockSpec((1, columns, half), lambda i: (i, 0, 0))],
        out_specs=pl.BlockSpec((2 * half, columns), lambda i: (i, 0)),
        out_shape=jax.ShapeDtypeStruct((sources * 2 * half, columns), jnp.int32),
        name="unpack",
    )(codes)


def local(raw_values, bin_edges, feature_column, bin_offset):
    bundles = lax.axis_size("bundle")
    features = feature_column.shape[0]
    held = bin_edges.shape[0]
    first = (lax.axis_index("rows") * bundles + lax.axis_index("bundle")) * held
    offsets = lax.dynamic_slice_in_dim(bin_offset, first, held, 0)
    tables = make_tables(bin_edges, offsets.astype(jnp.float32)[:, None])
    tables = lax.all_gather(tables, ("rows", "bundle"), axis=0, tiled=True)
    codes = bin_rows(feature_column, raw_values, tables)
    codes = codes.reshape(bundles, features // bundles, codes.shape[1])
    codes = lax.all_to_all(codes, "bundle", split_axis=0, concat_axis=0, tiled=True)
    return unpack(codes)


def solution(mesh):
    in_specs = (P(("rows", "bundle"), None), P(("rows", "bundle"), None), P(), P())
    out_specs = P("rows", "bundle")
    return jax.shard_map(local, mesh=mesh, in_specs=in_specs, out_specs=out_specs, check_vma=False)
```

time: 273 us -> 157 us (0.58)
  other arithmetic: 139 us -> 0.76 us
  local copies, waits for them, and re-layouts: 61.4 us -> 2.3 us
  Pallas kernels: 0 us -> 44.8 us
  blocking collectives: 0 us -> 30.9 us
  waiting for transfers between devices: 53.2 us -> 64.6 us
  starting transfers between devices: 5.2 us -> 0.01 us
    reduce_sum x4 -> x0, other arithmetic: 130 us -> none  [one_block(): jnp.sum(part_rows[:, :, None] > edges[None, :, :], axis=2, dtype=jnp.int32)]
    all_gather x1, waiting for transfers between devices: 0.01 us -> 64.6 us  [local(): tables = lax.all_gather(tables, ('rows', 'bundle'), axis=0, tiled=True)]
    all_to_all x1 -> x0, waiting for transfers between devices: 52.5 us -> none  [local(): lax.all_to_all(ordered, 'bundle', split_axis=1, concat_axis=0, tiled=True)]
    pallas_call x0 -> x3, Pallas kernels: none -> 44.8 us  [the longest x1 36.7 us: bin_rows(): pl.pallas_call(bin_kernel, grid_spec=pltpu.PrefetchScalarGridSpec(num_sca...]
    all_to_all x0 -> x1, blocking collectives: none -> 30.9 us  [local(): lax.all_to_all(codes, 'bundle', split_axis=0, concat_axis=0, tiled=True)]
    gather x3 -> x0, local copies, waits for them, and re-layouts: 25.3 us -> none  [the longest x1 18.4 us: local(): ordered = jnp.take(raw_values, owner_feature, axis=1)]
    scatter x1 -> x0, local copies, waits for them, and re-layouts: 15.5 us -> none  [local(): owner_feature = jnp.zeros((count_feat,), jnp.int32).at[feature_column].se...]
    unnamed x5 -> x0, local copies, waits for them, and re-layouts: 5.61 us -> none
  transfers between devices with their start and end apart: 2 -> 1, of which waited for: 1 -> 1; matrix products, arithmetic and copies ran while one was open for 19% -> 0% of each run, Pallas kernels for 0% -> 0%
where the time goes in v1:
time: 157 us
  waiting for transfers between devices  64.6 us (41%)
  Pallas kernels  44.8 us (29%)
  blocking collectives  30.9 us (20%)
  between operations  13.4 us (9%)
  local copies, waits for them, and re-layouts  2.3 us (1%)
    all_gather x1, waiting for transfers between devices, local(): tables = lax.all_gather(tables, ('rows', 'bundle'), axis=0, tiled=True)  64.6 us
    pallas_call x1, Pallas kernels, bin_rows(): pl.pallas_call(bin_kernel, grid_spec=pltpu.PrefetchScalarGridSpec(num_sca...  36.7 us
    all_to_all x1, blocking collectives, local(): lax.all_to_all(codes, 'bundle', split_axis=0, concat_axis=0, tiled=True)  30.9 us
    pallas_call x1, Pallas kernels, unpack(): pl.pallas_call(unpack_kernel, grid=(sources,), in_specs=[pl.BlockSpec((1,...  6.37 us
  transfers between devices with their start and end apart: 1, of which 1 were waited for; matrix products, arithmetic and copies ran while one was open for 0% of the time, Pallas kernels for 0%

profile of v1, /device:TPU:0, one launch (start us, length us, event | category | flops | bytes accessed | tf_op | source)
XLA Modules:
  0.0 156.7 jit_solution(2704659744212434794)
XLA Ops:
  6.5 0.0 all-gather.2.cloned.1.call-start
  6.5 0.8 convert_bitcast_fusion
  7.3 0.7 copy.5.offset_ref
  8.0 1.6 %pad.4.edges_ref = f32[128,256]{1,0:T(8,128)} pad(f32[128,255]{1,0:T(8,128)} %param.5, f32[]{:T(128)} %constant.4.clone.1), padding=0_0x0_1 | pad | bytes 261636 | tf_op jit(solution)/shard_map/jit(_pad)/pad | solution.py:41
  9.6 1.7 %make_tables.1 = f32[128,256]{1,0:T(8,128)} custom-call(f32[128,256]{1,0:T(8,128)} %pad.4.edges_ref, f32[128,1]{1,0:T(8,128)} %copy.5.offset_ref), custom_call_target="tpu_custom_call" | custom-call | tf_op jit(solution)/shard_map/make_tables/pallas_call | solution.py:37
  11.3 0.0 all-gather.2.cloned.1.call-update
  11.3 64.6 %all-gather.2.cloned.1.call-done.table_ref = f32[4096,256]{1,0:T(8,128)} async-done(((f32[128,256]{1,0:T(8,128)}), f32[4096,256]{1,0:T(8,128)}) %all-gather.2.cloned.1.call-update) | async-done | bytes 4194320 | tf_op jit(solution)/shard_map/all_gather | solution.py:113
  75.9 36.7 %bin_rows.1 = s32[4096,128]{1,0:T(8,128)} custom-call(s32[4096]{0:T(1024)} %column_ref.1, f32[256,4096]{1,0:T(8,128)} %raw_ref.1, f32[4096,256]{1,0:T(8,128)} %all-gather.2.cloned.1.call-done.table_ref), custom_call_target="tpu_custom_call" | custom-call | tf_op jit(solution)/shard_map/bin_rows/pallas_call | solution.py:71
  112.6 30.9 %all_to_all.5.code_ref = s32[8,512,128]{2,1,0:T(8,128)} all-to-all(s32[8,512,128]{2,1,0:T(8,128)} %bitcast.3), channel_id=1, replica_groups=mesh['rows'=4,'bundle'=8] {'bundle'}, dimensions={0} | all-to-all | bytes 4194304 | tf_op jit(solution)/shard_map/all_to_all | solution.py:116
  143.5 6.4 %unpack.1 = s32[2048,512]{1,0:T(8,128)} custom-call(s32[8,512,128]{2,1,0:T(8,128)} %all_to_all.5.code_ref), custom_call_target="tpu_custom_call" | custom-call | tf_op jit(solution)/shard_map/unpack/pallas_call | solution.py:96
Async XLA Ops:
  6.5 69.4 %all-gather.2.cloned.1.call-start = ((), (), s32[]{:S(2)}) async-start(), calls=%async_computation.1 | async-start | bytes 4325376 | tf_op jit(solution)/shard_map/all_gather | solution.py:113
Sparse Core Ops, SparseCore 0:
  11.4 64.4 all-gather.1

commit v2 on v1

--- a/solution.py
+++ b/solution.py
@@ -8,6 +8,7 @@
 from jax.sharding import PartitionSpec as P
 
 LANES = 128
+MESH = pl.DeviceIdType.MESH
 
 
 def lane_gather(table, index):
@@ -39,6 +40,121 @@
         out_shape=jax.ShapeDtypeStruct((count, 2 * LANES), jnp.float32),
         name="make_tables",
     )(jnp.pad(edges, ((0, 0), (0, 2 * LANES - edges.shape[1]))), offsets)
+
+
+def gather_kernel(table_ref, all_ref, send_sem, row_sem, side_sem, relay_sem, partner_sem):
+    held = table_ref.shape[0]
+    rows, bundles = lax.axis_size("rows"), lax.axis_size("bundle")
+    row, bundle = lax.axis_index("rows"), lax.axis_index("bundle")
+    sides = bundles // 2
+    partner = bundle + 1 - 2 * lax.rem(bundle, 2)
+    side = [lax.rem(bundle + 2 * step, bundles) for step in range(sides)]
+    source = [lax.rem(bundle + bundles - 2 * step, bundles) for step in range(sides)]
+    group = [lax.rem(row + step, rows) for step in range(rows)]
+    origin = [lax.rem(row + rows - step, rows) for step in range(rows)]
+    square = sides == 4
+    if square:
+        pair = lax.div(bundle, 2)
+        across = bundle + 2 - 4 * lax.rem(pair, 2)
+        along = bundle + 4 - 8 * lax.div(pair, 2)
+        corner = across + 4 - 8 * lax.div(pair, 2)
+
+    barrier = pltpu.get_barrier_semaphore()
+    others = [(peer, bundle) for peer in group[1:]] + [(row, partner)]
+    others += [(row, across), (row, along)] if square else [(row, peer) for peer in side[1:]]
+    for peer in others:
+        pl.semaphore_signal(barrier, inc=1, device_id=peer, device_id_type=MESH)
+    pl.semaphore_wait(barrier, len(others))
+
+    def at(row_index, bundle_index, start=0, size=held):
+        first = (row_index * bundles + bundle_index) * held + start
+        return all_ref.at[pl.ds(pl.multiple_of(first, 8), size)]
+
+    sent = []
+
+    def send(block, source_ref, device, arrival):
+        copy = pltpu.make_async_remote_copy(
+            src_ref=source_ref,
+            dst_ref=block,
+            send_sem=send_sem.at[len(sent)],
+            recv_sem=arrival,
+            device_id=device,
+            device_id_type=MESH,
+        )
+        copy.start()
+        sent.append(copy)
+
+    def arrived(block, arrival):
+        pltpu.make_async_copy(block, block, arrival).wait()
+
+    for step in range(1, rows):
+        send(at(row, bundle), table_ref, (group[step], bundle), row_sem.at[step])
+    all_ref[pl.ds(pl.multiple_of((row * bundles + bundle) * held, 8), held), :] = table_ref[...]
+    half = held // 2
+    for step in range(rows):
+        block = at(origin[step], bundle)
+        if step:
+            arrived(block, row_sem.at[step])
+        from_ref = block if step else table_ref
+        if square:
+            send(block, from_ref, (row, across), side_sem.at[step, 1])
+            send(block, from_ref, (row, along), side_sem.at[step, 2])
+        else:
+            for turn in range(1, sides):
+                send(block, from_ref, (row, side[turn]), side_sem.at[step, turn])
+        send(block, from_ref, (row, partner), partner_sem.at[step, 0])
+    for step in range(rows):
+        if square:
+            block = at(origin[step], across)
+            arrived(block, side_sem.at[step, 1])
+            tail = at(origin[step], across, half, half)
+            send(tail, tail, (row, along), relay_sem.at[step, 1])
+            send(block, block, (row, partner), partner_sem.at[step, 1])
+            block = at(origin[step], along)
+            arrived(block, side_sem.at[step, 2])
+            head = at(origin[step], along, 0, half)
+            send(head, head, (row, across), relay_sem.at[step, 0])
+            send(block, block, (row, partner), partner_sem.at[step, 2])
+        else:
+            for turn in range(1, sides):
+                block = at(origin[step], source[turn])
+                arrived(block, side_sem.at[step, turn])
+                send(block, block, (row, partner), partner_sem.at[step, turn])
+    if square:
+        for step in range(rows):
+            arrived(at(origin[step], corner, 0, half), relay_sem.at[step, 0])
+            arrived(at(origin[step], corner, half, half), relay_sem.at[step, 1])
+            block = at(origin[step], corner)
+            send(block, block, (row, partner), partner_sem.at[step, 3])
+    opposite = [partner] + ([across, along, corner] if square else source[1:])
+    for step in range(rows):
+        for turn in range(sides):
+            mate = partner if turn == 0 else opposite[turn] + 1 - 2 * lax.rem(bundle, 2)
+            arrived(at(origin[step], mate), partner_sem.at[step, turn])
+    for copy in sent:
+        copy.wait_send()
+
+
+def gather_tables(tables):
+    held, width = tables.shape
+    rows, bundles = lax.axis_size("rows"), lax.axis_size("bundle")
+    sides = bundles // 2
+    sends = rows - 1 + rows * 3 * sides
+    return pl.pallas_call(
+        gather_kernel,
+        out_shape=jax.ShapeDtypeStruct((rows * bundles * held, width), jnp.float32),
+        in_specs=[pl.BlockSpec(memory_space=pltpu.VMEM)],
+        out_specs=pl.BlockSpec(memory_space=pltpu.VMEM),
+        scratch_shapes=[
+            pltpu.SemaphoreType.DMA((sends,)),
+            pltpu.SemaphoreType.DMA((rows,)),
+            pltpu.SemaphoreType.DMA((rows, sides)),
+            pltpu.SemaphoreType.DMA((rows, 2)),
+            pltpu.SemaphoreType.DMA((rows, sides)),
+        ],
+        compiler_params=pltpu.CompilerParams(collective_id=0, has_side_effects=True),
+        name="gather_tables",
+    )(tables)
 
 
 def bin_kernel(column_ref, raw_ref, table_ref, code_ref):
@@ -110,7 +226,7 @@
     first = (lax.axis_index("rows") * bundles + lax.axis_index("bundle")) * held
     offsets = lax.dynamic_slice_in_dim(bin_offset, first, held, 0)
     tables = make_tables(bin_edges, offsets.astype(jnp.float32)[:, None])
-    tables = lax.all_gather(tables, ("rows", "bundle"), axis=0, tiled=True)
+    tables = gather_tables(tables)
     codes = bin_rows(feature_column, raw_values, tables)
     codes = codes.reshape(bundles, features // bundles, codes.shape[1])
     codes = lax.all_to_all(codes, "bundle", split_axis=0, concat_axis=0, tiled=True)

time: 157 us -> 111 us (0.71)
  waiting for transfers between devices: 64.6 us -> 0 us
  Pallas kernels: 44.8 us -> 76.8 us
  between operations: 13.4 us -> 0.01 us
    all_gather x1 -> x0, waiting for transfers between devices: 64.6 us -> none  [local(): tables = lax.all_gather(tables, ('rows', 'bundle'), axis=0, tiled=True)]
    pallas_call x0 -> x1, Pallas kernels: none -> 32.1 us  [gather_tables(): pl.pallas_call(gather_kernel, out_shape=jax.ShapeDtypeStruct((rows * bund...]
  transfers between devices with their start and end apart: 1 -> 0, of which waited for: 1 -> 0; matrix products, arithmetic and copies ran while one was open for 0% -> 0% of each run, Pallas kernels for 0% -> 0%
where the time goes in v2:
time: 111 us
  Pallas kernels  76.8 us (69%)
  blocking collectives  30.9 us (28%)
  local copies, waits for them, and re-layouts  2.3 us (2%)
    pallas_call x1, Pallas kernels, bin_rows(): pl.pallas_call(bin_kernel, grid_spec=pltpu.PrefetchScalarGridSpec(num_sca...  36.7 us
    pallas_call x1, Pallas kernels, gather_tables(): pl.pallas_call(gather_kernel, out_shape=jax.ShapeDtypeStruct((rows * bund...  32.1 us
    all_to_all x1, blocking collectives, local(): lax.all_to_all(codes, 'bundle', split_axis=0, concat_axis=0, tiled=True)  30.9 us
    pallas_call x1, Pallas kernels, unpack(): pl.pallas_call(unpack_kernel, grid=(sources,), in_specs=[pl.BlockSpec((1,...  6.37 us

profile of v2, /device:TPU:0, one launch (start us, length us, event | category | flops | bytes accessed | tf_op | source)
XLA Modules:
  0.0 110.8 jit_solution(12236141054218771390)
XLA Ops:
  0.0 0.8 convert_bitcast_fusion
  0.8 0.7 copy.5.offset_ref
  1.5 1.6 %pad.4.edges_ref = f32[128,256]{1,0:T(8,128)} pad(f32[128,255]{1,0:T(8,128)} %param.5, f32[]{:T(128)} %constant.4.clone.1), padding=0_0x0_1 | pad | bytes 261636 | tf_op jit(solution)/shard_map/jit(_pad)/pad | solution.py:42
  3.1 1.7 %make_tables.1.table_ref = f32[128,256]{1,0:T(8,128)} custom-call(f32[128,256]{1,0:T(8,128)} %pad.4.edges_ref, f32[128,1]{1,0:T(8,128)} %copy.5.offset_ref), custom_call_target="tpu_custom_call" | custom-call | tf_op jit(solution)/shard_map/make_tables/pallas_call | solution.py:38
  4.8 32.1 %gather_tables.1.table_ref = f32[4096,256]{1,0:T(8,128)} custom-call(f32[128,256]{1,0:T(8,128)} %make_tables.1.table_ref), custom_call_target="tpu_custom_call" | custom-call | tf_op jit(solution)/shard_map/gather_tables/pallas_call | solution.py:143
  36.8 36.7 %bin_rows.1 = s32[4096,128]{1,0:T(8,128)} custom-call(s32[4096]{0:T(1024)} %column_ref.1, f32[256,4096]{1,0:T(8,128)} %raw_ref.1, f32[4096,256]{1,0:T(8,128)} %gather_tables.1.table_ref), custom_call_target="tpu_custom_call" | custom-call | tf_op jit(solution)/shard_map/bin_rows/pallas_call | solution.py:187
  73.5 30.9 %all_to_all.5.code_ref = s32[8,512,128]{2,1,0:T(8,128)} all-to-all(s32[8,512,128]{2,1,0:T(8,128)} %bitcast.3), channel_id=1, replica_groups=mesh['rows'=4,'bundle'=8] {'bundle'}, dimensions={0} | all-to-all | bytes 4194304 | tf_op jit(solution)/shard_map/all_to_all | solution.py:232
  104.4 6.4 %unpack.1 = s32[2048,512]{1,0:T(8,128)} custom-call(s32[8,512,128]{2,1,0:T(8,128)} %all_to_all.5.code_ref), custom_call_target="tpu_custom_call" | custom-call | tf_op jit(solution)/shard_map/unpack/pallas_call | solution.py:212

commit v3 on v2

--- a/solution.py
+++ b/solution.py
@@ -8,29 +8,37 @@
 from jax.sharding import PartitionSpec as P
 
 LANES = 128
+BLOCK = 128
 MESH = pl.DeviceIdType.MESH
 
 
 def lane_gather(table, index):
-    return jnp.take_along_axis(table, index, axis=1, mode="promise_in_bounds")
+    return lax.gather(
+        table,
+        index[:, :, None],
+        lax.GatherDimensionNumbers(
+            offset_dims=(),
+            collapsed_slice_dims=(1,),
+            start_index_map=(1,),
+            operand_batching_dims=(0,),
+            start_indices_batching_dims=(0,),
+        ),
+        slice_sizes=(1, 1),
+        mode=lax.GatherScatterMode.PROMISE_IN_BOUNDS,
+    )
 
 
 def table_kernel(edges_ref, offset_ref, table_ref):
-    low, high = edges_ref[:, :LANES], edges_ref[:, LANES:]
+    edges = edges_ref[...]
+    tail = jnp.broadcast_to(offset_ref[...].astype(jnp.float32), (edges.shape[0], 2 * LANES - edges.shape[1]))
+    low = edges[:, :LANES]
+    high = jnp.concatenate([edges[:, LANES:], tail], axis=1)
     lane = lax.broadcasted_iota(jnp.int32, low.shape, 1)
-    edge = jnp.zeros_like(lane)
-    for level in range(7):
-        width = 1 << level
-        at_level = (lane >= width) & (lane < 2 * width)
-        edge = jnp.where(at_level, (2 * (lane - width) + 1) * (LANES // width) - 1, edge)
-
-    def pick(index):
+    for start in range(2):
+        index = 2 * lane + 1 - start
         inner = index & (LANES - 1)
-        return jnp.where(index < LANES, lane_gather(low, inner), lane_gather(high, inner))
-
-    offset = jnp.broadcast_to(offset_ref[...], low.shape)
-    table_ref[:, :LANES] = jnp.where(lane == 0, offset, pick(edge))
-    table_ref[:, LANES:] = pick(2 * lane)
+        picked = jnp.where(index < LANES, lane_gather(low, inner), lane_gather(high, inner))
+        table_ref[:, start * LANES : (start + 1) * LANES] = picked
 
 
 def make_tables(edges, offsets):
@@ -39,7 +47,7 @@
         table_kernel,
         out_shape=jax.ShapeDtypeStruct((count, 2 * LANES), jnp.float32),
         name="make_tables",
-    )(jnp.pad(edges, ((0, 0), (0, 2 * LANES - edges.shape[1]))), offsets)
+    )(edges, offsets)
 
 
 def gather_kernel(table_ref, all_ref, send_sem, row_sem, side_sem, relay_sem, partner_sem):
@@ -157,33 +165,36 @@
     )(tables)
 
 
+def bin_codes_of(values, table):
+    odd, even = table[:, :LANES], table[:, LANES:]
+    middle = LANES // 2 - 1
+    root = jnp.broadcast_to(odd[:, middle : middle + 1], odd.shape)
+    halves = []
+    for half in range(2):
+        x = values[:, half * LANES : (half + 1) * LANES]
+        step = LANES // 4
+        at = jnp.where(x > root, middle + step, middle - step)
+        while step > 1:
+            step //= 2
+            at = at + jnp.where(x > lane_gather(odd, at), step, -step)
+        at = at + jnp.where(x > lane_gather(odd, at), 1, 0)
+        halves.append(at + at + jnp.where(x > lane_gather(even, at), 1, 0))
+    offset = jnp.broadcast_to(odd[:, LANES - 1 :], odd.shape).astype(jnp.int32)
+    low, high = halves[0] + offset, halves[1] + offset
+    return low | (high << 16)
+
+
 def bin_kernel(column_ref, raw_ref, table_ref, code_ref):
     features = raw_ref.shape[1]
     first = pl.program_id(0) * features
-    group = 64
-    for start in range(0, features, group):
-        values = raw_ref[:, start : start + group].T
-        tree = table_ref[start : start + group, :LANES]
-        leaves = table_ref[start : start + group, LANES:]
-        root = jnp.broadcast_to(tree[:, 1:2], tree.shape)
-        halves = []
-        for half in range(2):
-            x = values[:, half * LANES : (half + 1) * LANES]
-            node = jnp.where(x > root, 3, 2)
-            for _ in range(6):
-                node = 2 * node + jnp.where(x > lane_gather(tree, node), 1, 0)
-            leaf = node - LANES
-            halves.append(2 * leaf + jnp.where(x > lane_gather(leaves, leaf), 1, 0))
-        offset = jnp.broadcast_to(tree[:, 0:1], tree.shape).astype(jnp.int32)
-        packed = halves[0] + halves[1] * 65536 + offset * 65537
-        for row in range(group):
-            column = column_ref[first + start + row]
-            code_ref[pl.ds(column, 1), :] = packed[row : row + 1, :]
+    packed = bin_codes_of(raw_ref[...].T, table_ref[...])
+    for row in range(features):
+        code_ref[pl.ds(column_ref[first + row], 1), :] = packed[row : row + 1, :]
 
 
 def bin_rows(column, raw, tables):
     rows, features = raw.shape
-    block = 128
+    block = BLOCK
     return pl.pallas_call(
         bin_kernel,
         grid_spec=pltpu.PrefetchScalarGridSpec(
@@ -225,7 +236,7 @@
     held = bin_edges.shape[0]
     first = (lax.axis_index("rows") * bundles + lax.axis_index("bundle")) * held
     offsets = lax.dynamic_slice_in_dim(bin_offset, first, held, 0)
-    tables = make_tables(bin_edges, offsets.astype(jnp.float32)[:, None])
+    tables = make_tables(bin_edges, offsets[:, None])
     tables = gather_tables(tables)
     codes = bin_rows(feature_column, raw_values, tables)
     codes = codes.reshape(bundles, features // bundles, codes.shape[1])

time: 111 us -> 106 us (0.955)
  Pallas kernels: 76.8 us -> 72.8 us
    pallas_call x1, Pallas kernels: 36.7 us -> 32.6 us  [bin_rows(): pl.pallas_call(bin_kernel, grid_spec=pltpu.PrefetchScalarGridSpec(num_sca...]
    pad x1 -> x0, local copies, waits for them, and re-layouts: 1.57 us -> none  [make_tables(): jnp.pad(edges, ((0, 0), (0, 2 * LANES - edges.shape[1])))]
where the time goes in v3:
time: 106 us; the launch traced here: 105 us
  Pallas kernels  72.8 us (69%)
  blocking collectives  30.9 us (29%)
  local copies, waits for them, and re-layouts  1.52 us (1%)
    pallas_call x1, Pallas kernels, bin_rows(): pl.pallas_call(bin_kernel, grid_spec=pltpu.PrefetchScalarGridSpec(num_sca...  32.6 us
    pallas_call x1, Pallas kernels, gather_tables(): pl.pallas_call(gather_kernel, out_shape=jax.ShapeDtypeStruct((rows * bund...  32.1 us
    all_to_all x1, blocking collectives, local(): lax.all_to_all(codes, 'bundle', split_axis=0, concat_axis=0, tiled=True)  30.9 us
    pallas_call x1, Pallas kernels, unpack(): pl.pallas_call(unpack_kernel, grid=(sources,), in_specs=[pl.BlockSpec((1,...  6.37 us

profile of v3, /device:TPU:0, one launch (start us, length us, event | category | flops | bytes accessed | tf_op | source)
XLA Modules:
  0.0 105.2 jit_solution(10223933622950518616)
XLA Ops:
  0.0 0.0 copy-start
  0.0 0.7 copy-done
  0.7 0.1 dynamic-slice_bitcast_fusion
  0.8 0.7 copy.5.offset_ref
  1.5 1.7 %make_tables.1.table_ref = f32[128,256]{1,0:T(8,128)} custom-call(f32[128,255]{1,0:T(8,128)} %edges_ref.1, s32[128,1]{1,0:T(8,128)} %copy.5.offset_ref), custom_call_target="tpu_custom_call" | custom-call | tf_op jit(solution)/shard_map/make_tables/pallas_call | solution.py:46
  3.3 32.1 %gather_tables.1.table_ref = f32[4096,256]{1,0:T(8,128)} custom-call(f32[128,256]{1,0:T(8,128)} %make_tables.1.table_ref), custom_call_target="tpu_custom_call" | custom-call | tf_op jit(solution)/shard_map/gather_tables/pallas_call | solution.py:151
  35.4 32.6 %bin_rows.1 = s32[4096,128]{1,0:T(8,128)} custom-call(s32[4096]{0:T(1024)} %column_ref.1, f32[256,4096]{1,0:T(8,128)} %raw_ref.1, f32[4096,256]{1,0:T(8,128)} %gather_tables.1.table_ref), custom_call_target="tpu_custom_call" | custom-call | tf_op jit(solution)/shard_map/bin_rows/pallas_call | solution.py:198
  67.9 30.9 %all_to_all.5.code_ref = s32[8,512,128]{2,1,0:T(8,128)} all-to-all(s32[8,512,128]{2,1,0:T(8,128)} %bitcast.3), channel_id=1, replica_groups=mesh['rows'=4,'bundle'=8] {'bundle'}, dimensions={0} | all-to-all | bytes 4194304 | tf_op jit(solution)/shard_map/all_to_all | solution.py:243
  98.8 6.4 %unpack.1 = s32[2048,512]{1,0:T(8,128)} custom-call(s32[8,512,128]{2,1,0:T(8,128)} %all_to_all.5.code_ref), custom_call_target="tpu_custom_call" | custom-call | tf_op jit(solution)/shard_map/unpack/pallas_call | solution.py:223
Async XLA Ops:
  0.0 0.7 copy-start

commit v4 on v3

v4 whole, which is shorter than its diff:
```python
import functools

import jax
import jax.numpy as jnp
from jax import lax
from jax.experimental import pallas as pl
from jax.experimental.pallas import tpu as pltpu
from jax.sharding import PartitionSpec as P

LANES = 128
BLOCK = 128
MESH = pl.DeviceIdType.MESH


def lane_gather(table, index):
    return lax.gather(
        table,
        index[:, :, None],
        lax.GatherDimensionNumbers(
            offset_dims=(),
            collapsed_slice_dims=(1,),
            start_index_map=(1,),
            operand_batching_dims=(0,),
            start_indices_batching_dims=(0,),
        ),
        slice_sizes=(1, 1),
        mode=lax.GatherScatterMode.PROMISE_IN_BOUNDS,
    )


def table_kernel(edges_ref, offset_ref, table_ref):
    edges = edges_ref[...]
    tail = jnp.broadcast_to(offset_ref[...].astype(jnp.float32), (edges.shape[0], 2 * LANES - edges.shape[1]))
    low = edges[:, :LANES]
    high = jnp.concatenate([edges[:, LANES:], tail], axis=1)
    lane = lax.broadcasted_iota(jnp.int32, low.shape, 1)
    for start in range(2):
        index = 2 * lane + 1 - start
        inner = index & (LANES - 1)
        picked = jnp.where(index < LANES, lane_gather(low, inner), lane_gather(high, inner))
        table_ref[:, start * LANES : (start + 1) * LANES] = picked


def make_tables(edges, offsets):
    count = edges.shape[0]
    return pl.pallas_call(
        table_kernel,
        out_shape=jax.ShapeDtypeStruct((count, 2 * LANES), jnp.float32),
        name="make_tables",
    )(edges, offsets)


def bin_codes_of(values, table):
    odd, even = table[:, :LANES], table[:, LANES:]
    middle = LANES // 2 - 1
    root = jnp.broadcast_to(odd[:, middle : middle + 1], odd.shape)
    halves = []
    for half in range(2):
        x = values[:, half * LANES : (half + 1) * LANES]
        step = LANES // 4
        at = jnp.where(x > root, middle + step, middle - step)
        while step > 1:
            step //= 2
            at = at + jnp.where(x > lane_gather(odd, at), step, -step)
        at = at + jnp.where(x > lane_gather(odd, at), 1, 0)
        halves.append(at + at + jnp.where(x > lane_gather(even, at), 1, 0))
    offset = jnp.broadcast_to(odd[:, LANES - 1 :], odd.shape).astype(jnp.int32)
    low, high = halves[0] + offset, halves[1] + offset
    return low | (high << 16)


def bin_kernel(
    table_ref, raw_hbm, code_ref, all_ref, raw_ref, values_ref, raw_sem, send_sem, row_sem, side_sem, relay_sem, partner_sem
):
    held = table_ref.shape[0]
    rows, bundles = lax.axis_size("rows"), lax.axis_size("bundle")
    row, bundle = lax.axis_index("rows"), lax.axis_index("bundle")
    sides = bundles // 2
    flip = 1 - 2 * lax.rem(bundle, 2)
    partner = bundle + flip
    group = [lax.rem(row + step, rows) for step in range(rows)]
    origin = [lax.rem(row + rows - step, rows) for step in range(rows)]
    square = sides == 4
    if square:
        pair = lax.div(bundle, 2)
        across = bundle + 2 - 4 * lax.rem(pair, 2)
        along = bundle + 4 - 8 * lax.div(pair, 2)
        corner = across + 4 - 8 * lax.div(pair, 2)
        target = [bundle, across, along]
        source = [bundle, across, along, corner]
    else:
        target = [lax.rem(bundle + 2 * step, bundles) for step in range(sides)]
        source = [lax.rem(bundle + bundles - 2 * step, bundles) for step in range(sides)]
    near = len(target)

    fetch = pltpu.make_async_copy(raw_hbm, raw_ref, raw_sem)
    fetch.start()
    barrier = pltpu.get_barrier_semaphore()
    others = [(peer, bundle) for peer in group[1:]] + [(row, peer) for peer in target[1:]] + [(row, partner)]
    for peer in others:
        pl.semaphore_signal(barrier, inc=1, device_id=peer, device_id_type=MESH)
    pl.semaphore_wait(barrier, len(others))

    def place(row_index, bundle_index):
        return (row_index * bundles + bundle_index) * held

    def at(row_index, bundle_index, start=0, size=held):
        first = place(row_index, bundle_index) + start
        return all_ref.at[pl.ds(pl.multiple_of(first, 8), size)]

    sent = []

    def send(block, source_ref, device, arrival):
        copy = pltpu.make_async_remote_copy(
            src_ref=source_ref,
            dst_ref=block,
            send_sem=send_sem.at[len(sent)],
            recv_sem=arrival,
            device_id=device,
            device_id_type=MESH,
        )
        copy.start()
        sent.append(copy)

    def arrived(block, arrival):
        pltpu.make_async_copy(block, block, arrival).wait()

    def use(blocks):
        firsts = [place(*block) for block in blocks]

        def body(index, carry):
            first = firsts[0]
            for other in range(1, len(firsts)):
                first = jnp.where(index == other, firsts[other], first)
            span = pl.ds(pl.multiple_of(first, 8), held)
            code_ref[span, :] = bin_codes_of(values_ref[span, :], all_ref[span, :])
            return carry

        lax.fori_loop(0, len(firsts), body, 0)

    half = held // 2
    for step in range(1, rows):
        send(at(row, bundle), table_ref, (group[step], bundle), row_sem.at[step])
    for stage in range(rows + 3):
        ready = []
        if stage < rows:
            block = at(origin[stage], bundle)
            if stage:
                arrived(block, row_sem.at[stage])
            from_ref = block if stage else table_ref
            for turn in range(1, near):
                send(block, from_ref, (row, target[turn]), side_sem.at[stage, turn])
            send(block, from_ref, (row, partner), partner_sem.at[stage, 0])
            ready.append((origin[stage], bundle))
        if stage == 0:
            all_ref[pl.ds(pl.multiple_of(place(row, bundle), 8), held), :] = table_ref[...]
            fetch.wait()

            def turn_over(index, carry):
                span = pl.ds(pl.multiple_of(index * LANES, LANES), LANES)
                values_ref[span, :] = raw_ref[:, span].T
                return carry

            lax.fori_loop(0, raw_ref.shape[1] // LANES, turn_over, 0)
        step = stage - 1
        if 0 <= step < rows:
            for turn in range(1, near):
                block = at(origin[step], source[turn])
                arrived(block, side_sem.at[step, turn])
                if square:
                    start = half * (2 - turn)
                    part = at(origin[step], source[turn], start, half)
                    send(part, part, (row, target[3 - turn]), relay_sem.at[step, 2 - turn])
                send(block, block, (row, partner), partner_sem.at[step, turn])
                ready.append((origin[step], source[turn]))
            arrived(at(origin[step], partner), partner_sem.at[step, 0])
            ready.append((origin[step], partner))
        step = stage - 2
        if 0 <= step < rows:
            if square:
                arrived(at(origin[step], corner, 0, half), relay_sem.at[step, 0])
                arrived(at(origin[step], corner, half, half), relay_sem.at[step, 1])
                block = at(origin[step], corner)
                send(block, block, (row, partner), partner_sem.at[step, 3])
                ready.append((origin[step], corner))
            for turn in range(1, near):
                arrived(at(origin[step], source[turn] + flip), partner_sem.at[step, turn])
                ready.append((origin[step], source[turn] + flip))
        step = stage - 3
        if 0 <= step < rows and square:
            arrived(at(origin[step], corner + flip), partner_sem.at[step, 3])
            ready.append((origin[step], corner + flip))
        if ready:
            use(ready)
    for copy in sent:
        copy.wait_send()


def bin_rows(tables, raw):
    held, width = tables.shape
    count, features = raw.shape
    rows, bundles = lax.axis_size("rows"), lax.axis_size("bundle")
    sides = bundles // 2
    sends = rows - 1 + rows * 3 * sides
    return pl.pallas_call(
        bin_kernel,
        out_shape=jax.ShapeDtypeStruct((features, count // 2), jnp.int32),
        in_specs=[pl.BlockSpec(memory_space=pltpu.VMEM), pl.BlockSpec(memory_space=pl.ANY)],
        out_specs=pl.BlockSpec(memory_space=pltpu.VMEM),
        scratch_shapes=[
            pltpu.VMEM((features, width), jnp.float32),
            pltpu.VMEM((count, features), jnp.float32),
            pltpu.VMEM((features, count), jnp.float32),
            pltpu.SemaphoreType.DMA,
            pltpu.SemaphoreType.DMA((sends,)),
            pltpu.SemaphoreType.DMA((rows,)),
            pltpu.SemaphoreType.DMA((rows, sides)),
            pltpu.SemaphoreType.DMA((rows, 2)),
            pltpu.SemaphoreType.DMA((rows, sides)),
        ],
        compiler_params=pltpu.CompilerParams(collective_id=0, has_side_effects=True),
        name="bin_rows",
    )(tables, raw)


def order_kernel(column_ref, code_ref, out_ref):
    features = code_ref.shape[0]
    first = pl.program_id(0) * features
    for row in range(features):
        out_ref[pl.ds(column_ref[first + row], 1), :] = code_ref[row : row + 1, :]


def order_columns(column, codes):
    features, width = codes.shape
    block = BLOCK
    return pl.pallas_call(
        order_kernel,
        grid_spec=pltpu.PrefetchScalarGridSpec(
            num_scalar_prefetch=1,
            grid=(features // block,),
            in_specs=[pl.BlockSpec((block, width), lambda i, c: (i, 0))],
            out_specs=pl.BlockSpec((features, width), lambda i, c: (0, 0)),
        ),
        out_shape=jax.ShapeDtypeStruct((features, width), jnp.int32),
        name="order_columns",
    )(column, codes)


def unpack_kernel(code_ref, out_ref):
    half = code_ref.shape[2]
    codes = code_ref[0].T
    out_ref[:half, :] = codes & 65535
    out_ref[half:, :] = codes >> 16


def unpack(codes):
    sources, columns, half = codes.shape
    return pl.pallas_call(
        unpack_kernel,
        grid=(sources,),
        in_specs=[pl.BlockSpec((1, columns, half), lambda i: (i, 0, 0))],
        out_specs=pl.BlockSpec((2 * half, columns), lambda i: (i, 0)),
        out_shape=jax.ShapeDtypeStruct((sources * 2 * half, columns), jnp.int32),
        name="unpack",
    )(codes)


def local(raw_values, bin_edges, feature_column, bin_offset):
    bundles = lax.axis_size("bundle")
    features = feature_column.shape[0]
    held = bin_edges.shape[0]
    first = (lax.axis_index("rows") * bundles + lax.axis_index("bundle")) * held
    offsets = lax.dynamic_slice_in_dim(bin_offset, first, held, 0)
    tables = make_tables(bin_edges, offsets[:, None])
    codes = order_columns(feature_column, bin_rows(tables, raw_values))
    codes = codes.reshape(bundles, features // bundles, codes.shape[1])
    codes = lax.all_to_all(codes, "bundle", split_axis=0, concat_axis=0, tiled=True)
    return unpack(codes)


def solution(mesh):
    in_specs = (P(("rows", "bundle"), None), P(("rows", "bundle"), None), P(), P())
    out_specs = P("rows", "bundle")
    return jax.shard_map(local, mesh=mesh, in_specs=in_specs, out_specs=out_specs, check_vma=False)
```

time: 106 us -> 102 us (0.962)
  the two profiles are of different devices: /device:TPU:0 before, /device:TPU:16 now
where the time goes in v4:
time: 102 us; the launch traced here: 101 us
  Pallas kernels  68.1 us (67%)
  blocking collectives  30.9 us (30%)
  local copies, waits for them, and re-layouts  1.52 us (1%)
    pallas_call x1, Pallas kernels, bin_rows(): pl.pallas_call(bin_kernel, out_shape=jax.ShapeDtypeStruct((features, coun...  42.3 us
    all_to_all x1, blocking collectives, local(): lax.all_to_all(codes, 'bundle', split_axis=0, concat_axis=0, tiled=True)  30.9 us
    pallas_call x1, Pallas kernels, order_columns(): pl.pallas_call(order_kernel, grid_spec=pltpu.PrefetchScalarGridSpec(num_s...  17.7 us
    pallas_call x1, Pallas kernels, unpack(): pl.pallas_call(unpack_kernel, grid=(sources,), in_specs=[pl.BlockSpec((1,...  6.37 us

profile of v4, /device:TPU:16, one launch (start us, length us, event | category | flops | bytes accessed | tf_op | source)
XLA Modules:
  0.0 100.5 jit_solution(7137580858210457900)
XLA Ops:
  0.0 0.0 copy-start
  0.0 0.7 copy-done
  0.7 0.1 dynamic-slice_bitcast_fusion
  0.8 0.7 copy.5.offset_ref
  1.5 1.7 %make_tables.1.table_ref = f32[128,256]{1,0:T(8,128)} custom-call(f32[128,255]{1,0:T(8,128)} %edges_ref.1, s32[128,1]{1,0:T(8,128)} %copy.5.offset_ref), custom_call_target="tpu_custom_call" | custom-call | tf_op jit(solution)/shard_map/make_tables/pallas_call | solution.py:46
  3.3 42.3 %bin_rows.1.code_ref = s32[4096,128]{1,0:T(8,128)} custom-call(f32[128,256]{1,0:T(8,128)} %make_tables.1.table_ref, f32[256,4096]{1,0:T(8,128)} %raw_hbm.1), custom_call_target="tpu_custom_call" | custom-call | tf_op jit(solution)/shard_map/bin_rows/pallas_call | solution.py:205
  45.6 17.7 %order_columns.1 = s32[4096,128]{1,0:T(8,128)} custom-call(s32[4096]{0:T(1024)} %column_ref.1, s32[4096,128]{1,0:T(8,128)} %bin_rows.1.code_ref), custom_call_target="tpu_custom_call" | custom-call | tf_op jit(solution)/shard_map/order_columns/pallas_call | solution.py:236
  63.2 30.9 %all_to_all.5.code_ref = s32[8,512,128]{2,1,0:T(8,128)} all-to-all(s32[8,512,128]{2,1,0:T(8,128)} %bitcast.3), channel_id=1, replica_groups=mesh['rows'=4,'bundle'=8] {'bundle'}, dimensions={0} | all-to-all | bytes 4194304 | tf_op jit(solution)/shard_map/all_to_all | solution.py:277
  94.1 6.4 %unpack.1 = s32[2048,512]{1,0:T(8,128)} custom-call(s32[8,512,128]{2,1,0:T(8,128)} %all_to_all.5.code_ref), custom_call_target="tpu_custom_call" | custom-call | tf_op jit(solution)/shard_map/unpack/pallas_call | solution.py:258
Async XLA Ops:
  0.0 0.7 copy-start

commit v5 on v4

--- a/solution.py
+++ b/solution.py
@@ -224,26 +224,75 @@
 
 
 def order_kernel(column_ref, code_ref, out_ref):
-    features = code_ref.shape[0]
-    first = pl.program_id(0) * features
-    for row in range(features):
-        out_ref[pl.ds(column_ref[first + row], 1), :] = code_ref[row : row + 1, :]
+    def body(index, carry):
+        first = pl.multiple_of(index * BLOCK, BLOCK)
+        codes = code_ref[pl.ds(first, BLOCK), :]
+        for row in range(BLOCK):
+            out_ref[pl.ds(column_ref[first + row], 1), :] = codes[row : row + 1, :]
+        return carry
+
+    lax.fori_loop(0, code_ref.shape[0] // BLOCK, body, 0)
 
 
 def order_columns(column, codes):
-    features, width = codes.shape
-    block = BLOCK
     return pl.pallas_call(
         order_kernel,
-        grid_spec=pltpu.PrefetchScalarGridSpec(
-            num_scalar_prefetch=1,
-            grid=(features // block,),
-            in_specs=[pl.BlockSpec((block, width), lambda i, c: (i, 0))],
-            out_specs=pl.BlockSpec((features, width), lambda i, c: (0, 0)),
-        ),
-        out_shape=jax.ShapeDtypeStruct((features, width), jnp.int32),
+        out_shape=jax.ShapeDtypeStruct(codes.shape, jnp.int32),
+        in_specs=[pl.BlockSpec(memory_space=pltpu.SMEM), pl.BlockSpec(memory_space=pltpu.VMEM)],
+        out_specs=pl.BlockSpec(memory_space=pltpu.VMEM),
         name="order_columns",
     )(column, codes)
+
+
+def exchange_kernel(code_ref, out_ref, own_ref, own_sem, send_sem, arrive_sem):
+    bundles = lax.axis_size("bundle")
+    row, bundle = lax.axis_index("rows"), lax.axis_index("bundle")
+    keep = pltpu.make_async_copy(code_ref.at[bundle], own_ref, own_sem)
+    keep.start()
+    barrier = pltpu.get_barrier_semaphore()
+    peers = [lax.rem(bundle + step, bundles) for step in range(bundles)]
+    for peer in peers[1:]:
+        pl.semaphore_signal(barrier, inc=1, device_id=(row, peer), device_id_type=MESH)
+    pl.semaphore_wait(barrier, bundles - 1)
+    sent = []
+    for step in range(1, bundles):
+        copy = pltpu.make_async_remote_copy(
+            src_ref=code_ref.at[peers[step]],
+            dst_ref=out_ref.at[bundle],
+            send_sem=send_sem.at[step],
+            recv_sem=arrive_sem.at[step],
+            device_id=(row, peers[step]),
+            device_id_type=MESH,
+        )
+        copy.start()
+        sent.append(copy)
+    keep.wait()
+    keep = pltpu.make_async_copy(own_ref, out_ref.at[bundle], own_sem)
+    keep.start()
+    for step in range(1, bundles):
+        block = out_ref.at[lax.rem(bundle + bundles - step, bundles)]
+        pltpu.make_async_copy(block, block, arrive_sem.at[step]).wait()
+    for copy in sent:
+        copy.wait_send()
+    keep.wait()
+
+
+def exchange(codes):
+    bundles, columns, width = codes.shape
+    return pl.pallas_call(
+        exchange_kernel,
+        out_shape=jax.ShapeDtypeStruct(codes.shape, jnp.int32),
+        in_specs=[pl.BlockSpec(memory_space=pl.ANY)],
+        out_specs=pl.BlockSpec(memory_space=pl.ANY),
+        scratch_shapes=[
+            pltpu.VMEM((columns, width), jnp.int32),
+            pltpu.SemaphoreType.DMA,
+            pltpu.SemaphoreType.DMA((bundles,)),
+            pltpu.SemaphoreType.DMA((bundles,)),
+        ],
+        compiler_params=pltpu.CompilerParams(collective_id=1, has_side_effects=True),
+        name="exchange",
+    )(codes)
 
 
 def unpack_kernel(code_ref, out_ref):
@@ -274,7 +323,7 @@
     tables = make_tables(bin_edges, offsets[:, None])
     codes = order_columns(feature_column, bin_rows(tables, raw_values))
     codes = codes.reshape(bundles, features // bundles, codes.shape[1])
-    codes = lax.all_to_all(codes, "bundle", split_axis=0, concat_axis=0, tiled=True)
+    codes = exchange(codes)
     return unpack(codes)
 
 

time: 102 us -> 85.5 us (0.84)
  the two profiles are of different devices: /device:TPU:16 before, /device:TPU:17 now
where the time goes in v5:
time: 85.5 us; the launch traced here: 85.2 us
  Pallas kernels  83.6 us (98%)
  local copies, waits for them, and re-layouts  1.52 us (2%)
    pallas_call x1, Pallas kernels, bin_rows(): pl.pallas_call(bin_kernel, out_shape=jax.ShapeDtypeStruct((features, coun...  40.7 us
    pallas_call x1, Pallas kernels, exchange(): pl.pallas_call(exchange_kernel, out_shape=jax.ShapeDtypeStruct(codes.shap...  28.5 us
    pallas_call x1, Pallas kernels, unpack(): pl.pallas_call(unpack_kernel, grid=(sources,), in_specs=[pl.BlockSpec((1,...  6.38 us
    pallas_call x1, Pallas kernels, order_columns(): pl.pallas_call(order_kernel, out_shape=jax.ShapeDtypeStruct(codes.shape,...  6.31 us
    pallas_call x1, Pallas kernels, make_tables(): pl.pallas_call(table_kernel, out_shape=jax.ShapeDtypeStruct((count, 2 * L...  1.74 us

profile of v5, /device:TPU:17, one launch (start us, length us, event | category | flops | bytes accessed | tf_op | source)
XLA Modules:
  0.0 85.2 jit_solution(5274553266283594382)
XLA Ops:
  0.0 0.0 copy-start
  0.0 0.7 copy-done
  0.7 0.1 dynamic-slice_bitcast_fusion
  0.8 0.7 copy.5.offset_ref
  1.5 1.7 %make_tables.1.table_ref = f32[128,256]{1,0:T(8,128)} custom-call(f32[128,255]{1,0:T(8,128)} %edges_ref.1, s32[128,1]{1,0:T(8,128)} %copy.5.offset_ref), custom_call_target="tpu_custom_call" | custom-call | tf_op jit(solution)/shard_map/make_tables/pallas_call | solution.py:46
  3.3 40.7 %bin_rows.1.code_ref = s32[4096,128]{1,0:T(8,128)} custom-call(f32[128,256]{1,0:T(8,128)} %make_tables.1.table_ref, f32[256,4096]{1,0:T(8,128)} %raw_hbm.1), custom_call_target="tpu_custom_call" | custom-call | tf_op jit(solution)/shard_map/bin_rows/pallas_call | solution.py:205
  44.0 6.3 %order_columns.1 = s32[4096,128]{1,0:T(8,128)} custom-call(s32[4096]{0:T(1024)} %column_ref.1, s32[4096,128]{1,0:T(8,128)} %bin_rows.1.code_ref), custom_call_target="tpu_custom_call" | custom-call | tf_op jit(solution)/shard_map/order_columns/pallas_call | solution.py:238
  50.3 28.5 %exchange.1.code_ref = s32[8,512,128]{2,1,0:T(8,128)} custom-call(s32[8,512,128]{2,1,0:T(8,128)} %bitcast.3), custom_call_target="tpu_custom_call" | custom-call | tf_op jit(solution)/shard_map/exchange/pallas_call | solution.py:282
  78.8 6.4 %unpack.1 = s32[2048,512]{1,0:T(8,128)} custom-call(s32[8,512,128]{2,1,0:T(8,128)} %exchange.1.code_ref), custom_call_target="tpu_custom_call" | custom-call | tf_op jit(solution)/shard_map/unpack/pallas_call | solution.py:307
Async XLA Ops:
  0.0 0.7 copy-start

commit v6 on v5

--- a/solution.py
+++ b/solution.py
@@ -28,9 +28,9 @@
     )
 
 
-def table_kernel(edges_ref, offset_ref, table_ref):
+def table_kernel(edges_ref, table_ref):
     edges = edges_ref[...]
-    tail = jnp.broadcast_to(offset_ref[...].astype(jnp.float32), (edges.shape[0], 2 * LANES - edges.shape[1]))
+    tail = jnp.zeros((edges.shape[0], 2 * LANES - edges.shape[1]), jnp.float32)
     low = edges[:, :LANES]
     high = jnp.concatenate([edges[:, LANES:], tail], axis=1)
     lane = lax.broadcasted_iota(jnp.int32, low.shape, 1)
@@ -41,13 +41,13 @@
         table_ref[:, start * LANES : (start + 1) * LANES] = picked
 
 
-def make_tables(edges, offsets):
+def make_tables(edges):
     count = edges.shape[0]
     return pl.pallas_call(
         table_kernel,
         out_shape=jax.ShapeDtypeStruct((count, 2 * LANES), jnp.float32),
         name="make_tables",
-    )(edges, offsets)
+    )(edges)
 
 
 def bin_codes_of(values, table):
@@ -64,9 +64,7 @@
             at = at + jnp.where(x > lane_gather(odd, at), step, -step)
         at = at + jnp.where(x > lane_gather(odd, at), 1, 0)
         halves.append(at + at + jnp.where(x > lane_gather(even, at), 1, 0))
-    offset = jnp.broadcast_to(odd[:, LANES - 1 :], odd.shape).astype(jnp.int32)
-    low, high = halves[0] + offset, halves[1] + offset
-    return low | (high << 16)
+    return halves[0] | (halves[1] << 16)
 
 
 def bin_kernel(
@@ -223,10 +221,11 @@
     )(tables, raw)
 
 
-def order_kernel(column_ref, code_ref, out_ref):
+def order_kernel(column_ref, offset_ref, code_ref, out_ref):
     def body(index, carry):
         first = pl.multiple_of(index * BLOCK, BLOCK)
-        codes = code_ref[pl.ds(first, BLOCK), :]
+        offset = jnp.broadcast_to(offset_ref[pl.ds(index, 1), :], (BLOCK, BLOCK)).T[:, : code_ref.shape[1]]
+        codes = code_ref[pl.ds(first, BLOCK), :] + (offset | (offset << 16))
         for row in range(BLOCK):
             out_ref[pl.ds(column_ref[first + row], 1), :] = codes[row : row + 1, :]
         return carry
@@ -234,14 +233,18 @@
     lax.fori_loop(0, code_ref.shape[0] // BLOCK, body, 0)
 
 
-def order_columns(column, codes):
+def order_columns(column, offset, codes):
     return pl.pallas_call(
         order_kernel,
         out_shape=jax.ShapeDtypeStruct(codes.shape, jnp.int32),
-        in_specs=[pl.BlockSpec(memory_space=pltpu.SMEM), pl.BlockSpec(memory_space=pltpu.VMEM)],
+        in_specs=[
+            pl.BlockSpec(memory_space=pltpu.SMEM),
+            pl.BlockSpec(memory_space=pltpu.VMEM),
+            pl.BlockSpec(memory_space=pltpu.VMEM),
+        ],
         out_specs=pl.BlockSpec(memory_space=pltpu.VMEM),
         name="order_columns",
-    )(column, codes)
+    )(column, offset.reshape(-1, BLOCK), codes)
 
 
 def exchange_kernel(code_ref, out_ref, own_ref, own_sem, send_sem, arrive_sem):
@@ -296,19 +299,22 @@
 
 
 def unpack_kernel(code_ref, out_ref):
-    half = code_ref.shape[2]
-    codes = code_ref[0].T
-    out_ref[:half, :] = codes & 65535
-    out_ref[half:, :] = codes >> 16
+    sources, _, half = code_ref.shape
+    for source in range(sources):
+        codes = code_ref[source].T
+        start = 2 * half * source
+        out_ref[start : start + half, :] = codes & 65535
+        out_ref[start + half : start + 2 * half, :] = codes >> 16
 
 
 def unpack(codes):
     sources, columns, half = codes.shape
+    block = 2
     return pl.pallas_call(
         unpack_kernel,
-        grid=(sources,),
-        in_specs=[pl.BlockSpec((1, columns, half), lambda i: (i, 0, 0))],
-        out_specs=pl.BlockSpec((2 * half, columns), lambda i: (i, 0)),
+        grid=(sources // block,),
+        in_specs=[pl.BlockSpec((block, columns, half), lambda i: (i, 0, 0))],
+        out_specs=pl.BlockSpec((block * 2 * half, columns), lambda i: (i, 0)),
         out_shape=jax.ShapeDtypeStruct((sources * 2 * half, columns), jnp.int32),
         name="unpack",
     )(codes)
@@ -317,11 +323,8 @@
 def local(raw_values, bin_edges, feature_column, bin_offset):
     bundles = lax.axis_size("bundle")
     features = feature_column.shape[0]
-    held = bin_edges.shape[0]
-    first = (lax.axis_index("rows") * bundles + lax.axis_index("bundle")) * held
-    offsets = lax.dynamic_slice_in_dim(bin_offset, first, held, 0)
-    tables = make_tables(bin_edges, offsets[:, None])
-    codes = order_columns(feature_column, bin_rows(tables, raw_values))
+    codes = bin_rows(make_tables(bin_edges), raw_values)
+    codes = order_columns(feature_column, bin_offset, codes)
     codes = codes.reshape(bundles, features // bundles, codes.shape[1])
     codes = exchange(codes)
     return unpack(codes)

time: 85.5 us -> 83.8 us (0.980)
  local copies, waits for them, and re-layouts: 1.52 us -> 0 us
    pallas_call x1, Pallas kernels: 6.31 us -> 8.26 us  [order_columns(): pl.pallas_call(order_kernel, out_shape=jax.ShapeDtypeStruct(codes.shape,...]
    pallas_call x1, Pallas kernels: 6.38 us -> 4.47 us  [unpack(): pl.pallas_call(unpack_kernel, grid=(sources // block,), in_specs=[pl.Bloc...]
where the time goes in v6:
time: 83.8 us; the launch traced here: 83.5 us
  Pallas kernels  83.5 us (100%)
    pallas_call x1, Pallas kernels, bin_rows(): pl.pallas_call(bin_kernel, out_shape=jax.ShapeDtypeStruct((features, coun...  40.6 us
    pallas_call x1, Pallas kernels, exchange(): pl.pallas_call(exchange_kernel, out_shape=jax.ShapeDtypeStruct(codes.shap...  28.5 us
    pallas_call x1, Pallas kernels, order_columns(): pl.pallas_call(order_kernel, out_shape=jax.ShapeDtypeStruct(codes.shape,...  8.26 us
    pallas_call x1, Pallas kernels, unpack(): pl.pallas_call(unpack_kernel, grid=(sources // block,), in_specs=[pl.Bloc...  4.47 us
    pallas_call x1, Pallas kernels, make_tables(): pl.pallas_call(table_kernel, out_shape=jax.ShapeDtypeStruct((count, 2 * L...  1.7 us

profile of v6, /device:TPU:17, one launch (start us, length us, event | category | flops | bytes accessed | tf_op | source)
XLA Modules:
  0.0 83.5 jit_solution(1928017840091188368)
XLA Ops:
  0.0 1.7 %make_tables.1.table_ref = f32[128,256]{1,0:T(8,128)} custom-call(f32[128,255]{1,0:T(8,128)} %edges_ref.1), custom_call_target="tpu_custom_call" | custom-call | tf_op jit(solution)/shard_map/make_tables/pallas_call | solution.py:46
  1.7 40.6 %bin_rows.1.code_ref = s32[4096,128]{1,0:T(8,128)} custom-call(f32[128,256]{1,0:T(8,128)} %make_tables.1.table_ref, f32[256,4096]{1,0:T(8,128)} %raw_hbm.1), custom_call_target="tpu_custom_call" | custom-call | tf_op jit(solution)/shard_map/bin_rows/pallas_call | solution.py:203
  42.3 8.3 %order_columns.1 = s32[4096,128]{1,0:T(8,128)} custom-call(s32[4096]{0:T(1024)} %column_ref.1, s32[32,128]{1,0:T(8,128)} %bitcast.3, s32[4096,128]{1,0:T(8,128)} %bin_rows.1.code_ref), custom_call_target="tpu_custom_call" | custom-call | tf_op jit(solution)/shard_map/order_columns/pallas_call | solution.py:237
  50.6 28.5 %exchange.1.code_ref = s32[8,512,128]{2,1,0:T(8,128)} custom-call(s32[8,512,128]{2,1,0:T(8,128)} %bitcast.2), custom_call_target="tpu_custom_call" | custom-call | tf_op jit(solution)/shard_map/exchange/pallas_call | solution.py:285
  79.1 4.5 %unpack.1 = s32[2048,512]{1,0:T(8,128)} custom-call(s32[8,512,128]{2,1,0:T(8,128)} %exchange.1.code_ref), custom_call_target="tpu_custom_call" | custom-call | tf_op jit(solution)/shard_map/unpack/pallas_call | solution.py:313
